TPU v7x, 32 devices: a whole 2x2x4 slice. The times are simulated.
32 devices in a mesh: gx: 2 (over y), gy: 4 (over z), gz: 4 (over x, core).
Axes of the slice: x: 2, y: 2, z: 4, core: 2. Of those that a mesh axis runs over, the one named last changes fastest.
Arguments:
- source: float32 [2, 8, 32, 512], P(None, 'gx', 'gy', 'gz'), may hold values from -6 to 6
- sigma_intra: float32 [3, 8, 32, 512], P(None, 'gx', 'gy', 'gz'), may hold values from 0.3 to 3
- sigma_extra: float32 [3, 8, 32, 512], P(None, 'gx', 'gy', 'gz'), may hold values from 0.5 to 3
- membrane: float32 [8, 32, 512], P('gx', 'gy', 'gz'), may hold values from 0.5 to 5
Outputs:
- solution: float32 [2, 8, 32, 512], P(None, 'gx', 'gy', 'gz')
- residual: float32 [2, 8, 32, 512], P(None, 'gx', 'gy', 'gz')
All inputs are finite; a program needn't handle non-finite values.
Results may differ from a plain program's by a relative error of at most 0.0009.
Values sent between devices are 32-bit elements; how exact they have to be, the bound alone decides.
A program may use at most 64 MiB of HBM per device.

v0:
```python
import jax
import jax.numpy as jnp
from jax import lax
from jax.sharding import PartitionSpec as P

KRYLOV = 10


highest = lax.Precision.HIGHEST


def extended(block, sides, width):
    for axis, dim in sides:
        count = lax.axis_size(axis)
        forward = [(i, i + 1) for i in range(count - 1)]
        backward = [(target, source) for source, target in forward]
        low = lax.ppermute(
            lax.slice_in_dim(block, block.shape[dim] - width, None, axis=dim), axis, forward
        )
        high = lax.ppermute(lax.slice_in_dim(block, 0, width, axis=dim), axis, backward)
        block = jnp.concatenate([low, block, high], axis=dim)
    return block


def shifted(padded_grid, spatial, offset):
    pieces = [slice(1, -1), slice(1, -1), slice(1, -1)]
    if offset > 0:
        pieces[spatial] = slice(2, None)
    else:
        pieces[spatial] = slice(None, -2)
    return padded_grid[tuple(pieces)]


def face_terms(padded_sigma):
    upper_faces = []
    lower_faces = []
    for spatial in range(3):
        component = padded_sigma[spatial]
        middle = component[1:-1, 1:-1, 1:-1]
        upper_faces.append(0.5 * (middle + shifted(component, spatial, 1)))
        lower_faces.append(0.5 * (middle + shifted(component, spatial, -1)))
    diagonal = upper_faces[0] + lower_faces[0]
    for spatial in range(1, 3):
        diagonal = diagonal + upper_faces[spatial] + lower_faces[spatial]
    return (upper_faces, lower_faces, diagonal)


def apply_laplace(faces, padded_field):
    upper_faces, lower_faces, diagonal = faces
    result = diagonal * padded_field[1:-1, 1:-1, 1:-1]
    for spatial in range(3):
        result = result - upper_faces[spatial] * shifted(padded_field, spatial, 1)
        result = result - lower_faces[spatial] * shifted(padded_field, spatial, -1)
    return result


def operate(intra_faces, extra_faces, membrane, padded_pair):
    joined = padded_pair[0] + padded_pair[1]
    shared = apply_laplace(intra_faces, joined)
    leading = membrane * padded_pair[0, 1:-1, 1:-1, 1:-1] + shared
    second = shared + apply_laplace(extra_faces, padded_pair[1])
    return jnp.stack([leading, second])


def inverse_blocks(intra_faces, extra_faces, membrane):
    intra_sum = intra_faces[2]
    extra_sum = extra_faces[2]
    determinant = membrane * intra_sum + membrane * extra_sum + intra_sum * extra_sum
    return jnp.stack(
        [
            (intra_sum + extra_sum) / determinant,
            -intra_sum / determinant,
            (membrane + intra_sum) / determinant,
        ]
    )


def precondition(inverse, pair):
    leading = inverse[0] * pair[0] + inverse[1] * pair[1]
    second = inverse[1] * pair[0] + inverse[2] * pair[1]
    return jnp.stack([leading, second])


def least_squares(hessenberg, start_norm):
    krylov = hessenberg.shape[1]
    rotated = hessenberg
    target = jnp.zeros((krylov + 1,), jnp.float32).at[0].set(start_norm)
    for column in range(krylov):
        pivot = rotated[column, column]
        lower_entry = rotated[column + 1, column]
        radius = jnp.sqrt(pivot * pivot + lower_entry * lower_entry)
        cosine = pivot / radius
        sine_value = lower_entry / radius
        row_top = cosine * rotated[column] + sine_value * rotated[column + 1]
        row_below = -sine_value * rotated[column] + cosine * rotated[column + 1]
        rotated = rotated.at[column].set(row_top).at[column + 1].set(row_below)
        leading = cosine * target[column] + sine_value * target[column + 1]
        second = -sine_value * target[column] + cosine * target[column + 1]
        target = target.at[column].set(leading).at[column + 1].set(second)
    coeffs = jnp.zeros((krylov,), jnp.float32)
    for column in range(krylov - 1, -1, -1):
        partial_sum = jnp.sum(rotated[column, column + 1 :] * coeffs[column + 1 :])
        coeffs = coeffs.at[column].set((target[column] - partial_sum) / rotated[column, column])
    return coeffs


def body(source, sigma_intra, sigma_extra, membrane):
    stacked = jnp.concatenate([sigma_intra, sigma_extra], 0)
    padded_sigma = extended(stacked, (("gx", 1), ("gy", 2), ("gz", 3)), 1)
    intra_faces = face_terms(padded_sigma[:3])
    extra_faces = face_terms(padded_sigma[3:])
    inverse = inverse_blocks(intra_faces, extra_faces, membrane)
    start_norm = jnp.sqrt(lax.psum(jnp.sum(source * source), ("gx", "gy", "gz")))
    basis = jnp.zeros((KRYLOV + 1,) + source.shape, jnp.float32).at[0].set(source / start_norm)
    hessenberg = jnp.zeros((KRYLOV + 1, KRYLOV), jnp.float32)
    for column in range(KRYLOV):
        solved = precondition(inverse, basis[column])
        padded_solved = extended(solved, (("gx", 1), ("gy", 2), ("gz", 3)), 1)
        applied = operate(intra_faces, extra_faces, membrane, padded_solved)
        flat_basis = basis[: column + 1].reshape(column + 1, -1)
        local_project = jnp.dot(flat_basis, applied.reshape(-1), precision=highest)
        project, total = lax.psum((local_project, jnp.sum(applied * applied)), ("gx", "gy", "gz"))
        applied = applied - jnp.dot(project, flat_basis, precision=highest).reshape(applied.shape)
        norm_sq = total - jnp.sum(project * project)
        new_norm = jnp.sqrt(norm_sq)
        basis = basis.at[column + 1].set(applied / new_norm)
        hessenberg = (
            hessenberg.at[: column + 1, column].set(project).at[column + 1, column].set(new_norm)
        )
    coeffs = least_squares(hessenberg, start_norm)
    combined = jnp.dot(coeffs, basis[:KRYLOV].reshape(KRYLOV, -1), precision=highest).reshape(
        source.shape
    )
    solution = precondition(inverse, combined)
    remainder = jnp.zeros((KRYLOV + 1,), jnp.float32).at[0].set(start_norm) - jnp.dot(
        hessenberg, coeffs, precision=highest
    )
    residual = jnp.dot(remainder, basis.reshape(KRYLOV + 1, -1), precision=highest).reshape(
        source.shape
    )
    return (solution, residual)


def solution(mesh):
    placed = (
        P(None, "gx", "gy", "gz"),
        P(None, "gx", "gy", "gz"),
        P(None, "gx", "gy", "gz"),
        P("gx", "gy", "gz"),
    )
    return jax.shard_map(
        body,
        mesh=mesh,
        in_specs=placed,
        out_specs=(P(None, "gx", "gy", "gz"), P(None, "gx", "gy", "gz")),
        check_vma=False,
    )
```

profile of v0, /device:TPU:0, one launch (start us, length us, event | category | flops | bytes accessed | tf_op | source)
XLA Modules:
  0.0 870.4 jit_solution(12704058043179545021)
XLA Ops:
  1.5 4.9 collective-permute-start
  8.3 41.9 %psum.147 = f32[]{:T(128)} all-reduce(f32[]{:T(128)} %multiply_reduce_fusion.11), channel_id=1, replica_groups=mesh['gx'=2,'gy'=4,'gz'=4] {'gx','gy','gz'}, use_global_device_ids=true, to_apply=%region_1.0 | all-reduce | flops 1 | bytes 8 | tf_op jit(solution)/shard_map/psum | solution.py:113
  101.4 39.6 %all-reduce.13 = (f32[]{:T(128)}, f32[1]{0:T(128)}) all-reduce(f32[]{:T(128)} %get-tuple-element.995, f32[1]{0:T(128)} %bitcast.15), channel_id=1, replica_groups=mesh['gx'=2,'gy'=4,'gz'=4] {'gx','gy','gz'}, use_global_device_ids=true, to_apply=%region_4.0 | all-reduce | flops 2 | bytes 16 | tf_op jit(solution)/shard_map/psum | solution.py:122
  143.7 4.4 collective-permute-start.12
  149.4 4.2 collective-permute-done.13
  171.2 39.8 %all-reduce.12 = (f32[2]{0:T(128)S(1)}, f32[]{:T(128)}) all-reduce(f32[2]{0:T(128)S(1)} %convolution_bitcast_fusion.9, f32[]{:T(128)} %get-tuple-element.1175), channel_id=1, replica_groups=mesh['gx'=2,'gy'=4,'gz'=4] {'gx','gy','gz'}, use_global_device_ids=true, to_apply=%region_6.0 | all-reduce | flops 3 | bytes 24 | tf_op jit(solution)/shard_map/psum | solution.py:122
  213.4 4.4 collective-permute-start.18
  240.8 39.8 %all-reduce.11 = (f32[3]{0:T(128)S(1)}, f32[]{:T(128)}) all-reduce(f32[3]{0:T(128)S(1)} %convolution_bitcast_fusion.8, f32[]{:T(128)} %get-tuple-element.1171), channel_id=1, replica_groups=mesh['gx'=2,'gy'=4,'gz'=4] {'gx','gy','gz'}, use_global_device_ids=true, to_apply=%region_11.0 | all-reduce | flops 4 | bytes 32 | tf_op jit(solution)/shard_map/psum | solution.py:122
  283.1 4.4 collective-permute-start.24
  288.9 4.2 collective-permute-done.25
  310.5 39.8 %all-reduce.10 = (f32[4]{0:T(128)S(1)}, f32[]{:T(128)}) all-reduce(f32[4]{0:T(128)S(1)} %convolution_bitcast_fusion.7, f32[]{:T(128)} %get-tuple-element.1167), channel_id=1, replica_groups=mesh['gx'=2,'gy'=4,'gz'=4] {'gx','gy','gz'}, use_global_device_ids=true, to_apply=%region_16.0 | all-reduce | flops 5 | bytes 40 | tf_op jit(solution)/shard_map/psum | solution.py:122
  352.6 4.4 collective-permute-start.30
  380.0 39.7 %all-reduce.9 = (f32[5]{0:T(128)S(1)}, f32[]{:T(128)}) all-reduce(f32[5]{0:T(128)S(1)} %convolution_bitcast_fusion.6, f32[]{:T(128)} %get-tuple-element.1163), channel_id=1, replica_groups=mesh['gx'=2,'gy'=4,'gz'=4] {'gx','gy','gz'}, use_global_device_ids=true, to_apply=%region_21.0 | all-reduce | flops 6 | bytes 48 | tf_op jit(solution)/shard_map/psum | solution.py:122
  422.0 4.4 collective-permute-start.36
  427.8 4.2 collective-permute-done.37
  449.4 39.8 %all-reduce.8 = (f32[6]{0:T(128)S(1)}, f32[]{:T(128)}) all-reduce(f32[6]{0:T(128)S(1)} %convolution_bitcast_fusion.5, f32[]{:T(128)} %get-tuple-element.1159), channel_id=1, replica_groups=mesh['gx'=2,'gy'=4,'gz'=4] {'gx','gy','gz'}, use_global_device_ids=true, to_apply=%region_26.0 | all-reduce | flops 7 | bytes 56 | tf_op jit(solution)/shard_map/psum | solution.py:122
  491.5 4.4 collective-permute-start.42
  518.9 41.7 %all-reduce.7 = (f32[7]{0:T(128)S(1)}, f32[]{:T(128)}) all-reduce(f32[7]{0:T(128)S(1)} %convolution_bitcast_fusion.4, f32[]{:T(128)} %get-tuple-element.1155), channel_id=1, replica_groups=mesh['gx'=2,'gy'=4,'gz'=4] {'gx','gy','gz'}, use_global_device_ids=true, to_apply=%region_31.0 | all-reduce | flops 8 | bytes 64 | tf_op jit(solution)/shard_map/psum | solution.py:122
  562.8 4.4 collective-permute-start.48
  588.3 41.8 %all-reduce.6 = (f32[8]{0:T(128)S(1)}, f32[]{:T(128)}) all-reduce(f32[8]{0:T(128)S(1)} %convolution_bitcast_fusion.3, f32[]{:T(128)} %get-tuple-element.1151), channel_id=1, replica_groups=mesh['gx'=2,'gy'=4,'gz'=4] {'gx','gy','gz'}, use_global_device_ids=true, to_apply=%region_36.0 | all-reduce | flops 9 | bytes 72 | tf_op jit(solution)/shard_map/psum | solution.py:122
  632.6 4.4 collective-permute-start.54
  658.1 43.4 %all-reduce.5 = (f32[9]{0:T(128)S(1)}, f32[]{:T(128)}) all-reduce(f32[9]{0:T(128)S(1)} %convolution_bitcast_fusion.2, f32[]{:T(128)} %get-tuple-element.1147), channel_id=1, replica_groups=mesh['gx'=2,'gy'=4,'gz'=4] {'gx','gy','gz'}, use_global_device_ids=true, to_apply=%region_41.0 | all-reduce | flops 10 | bytes 80 | tf_op jit(solution)/shard_map/psum | solution.py:122
  704.0 4.4 collective-permute-start.60
  729.6 42.2 %all-reduce.4 = (f32[10]{0:T(128)S(1)}, f32[]{:T(128)}) all-reduce(f32[10]{0:T(128)S(1)} %convolution_bitcast_fusion.1, f32[]{:T(128)} %get-tuple-element.1143), channel_id=1, replica_groups=mesh['gx'=2,'gy'=4,'gz'=4] {'gx','gy','gz'}, use_global_device_ids=true, to_apply=%region_46.0 | all-reduce | flops 11 | bytes 88 | tf_op jit(solution)/shard_map/psum | solution.py:122
  (472 shorter events, 282.3 us)
Async XLA Ops:
  1.5 54.1 %collective-permute-start = (f32[6,1,8,128]{3,2,1,0:T(8,128)S(1)}, f32[6,1,8,128]{3,2,1,0:T(8,128)S(1)}, u32[]{:S(2)}, u32[]{:S(2)}) collective-permute-start(f32[6,1,8,128]{3,2,1,0:T(8,128)S(1)} %get-tuple-element.1101), channel_id=1, source_target_pairs={{0,16},{1,17},{2,18},{3,19},{4,20},{5,21},{6,22},{7,23},{8,24},{9,... | collective-permute-start | bytes 73736 | tf_op jit(solution)/shard_map/ppermute | solution.py:17
  7.0 48.6 %collective-permute-start.1 = (f32[6,1,8,128]{3,2,1,0:T(8,128)S(1)}, f32[6,1,8,128]{3,2,1,0:T(8,128)S(1)}, u32[]{:S(2)}, u32[]{:S(2)}) collective-permute-start(f32[6,1,8,128]{3,2,1,0:T(8,128)S(1)} %get-tuple-element.1102), channel_id=1, source_target_pairs={{16,0},{17,1},{18,2},{19,3},{20,4},{21,5},{22,6},{23,7},{24,8},{25... | collective-permute-start | bytes 73736 | tf_op jit(solution)/shard_map/ppermute | solution.py:20
  59.1 5.7 collective-permute-start.3
  66.3 6.0 collective-permute-start.5
  90.8 6.1 collective-permute-start.10
  143.7 5.7 collective-permute-start.12
  213.4 6.3 collective-permute-start.18
  217.7 5.5 collective-permute-start.19
  283.1 5.8 collective-permute-start.24
  287.5 5.5 collective-permute-start.25
  352.6 6.3 collective-permute-start.30
  422.0 5.8 collective-permute-start.36
  426.4 5.5 collective-permute-start.37
  432.0 6.5 collective-permute-start.38
  491.5 9.2 %collective-permute-start.42 = (f32[2,1,8,128]{3,2,1,0:T(8,128)S(1)}, f32[2,1,8,128]{3,2,1,0:T(8,128)S(1)}, u32[]{:S(2)}, u32[]{:S(2)}) collective-permute-start(f32[2,1,8,128]{3,2,1,0:T(8,128)S(1)} %get-tuple-element.1157), channel_id=1, source_target_pairs={{0,16},{1,17},{2,18},{3,19},{4,20},{5,21},{6,22},{7,23},{8,24},{9,... | collective-permute-start | bytes 24584 | tf_op jit(solution)/shard_map/ppermute | solution.py:17
  495.9 5.5 collective-permute-start.43
  501.5 6.5 collective-permute-start.44
  562.8 9.3 %collective-permute-start.48 = (f32[2,1,8,128]{3,2,1,0:T(8,128)S(1)}, f32[2,1,8,128]{3,2,1,0:T(8,128)S(1)}, u32[]{:S(2)}, u32[]{:S(2)}) collective-permute-start(f32[2,1,8,128]{3,2,1,0:T(8,128)S(1)} %get-tuple-element.1153), channel_id=1, source_target_pairs={{0,16},{1,17},{2,18},{3,19},{4,20},{5,21},{6,22},{7,23},{8,24},{9,... | collective-permute-start | bytes 24584 | tf_op jit(solution)/shard_map/ppermute | solution.py:17
  567.1 5.5 collective-permute-start.49
  572.7 6.6 collective-permute-start.50
  632.6 9.4 %collective-permute-start.54 = (f32[2,1,8,128]{3,2,1,0:T(8,128)S(1)}, f32[2,1,8,128]{3,2,1,0:T(8,128)S(1)}, u32[]{:S(2)}, u32[]{:S(2)}) collective-permute-start(f32[2,1,8,128]{3,2,1,0:T(8,128)S(1)} %get-tuple-element.1149), channel_id=1, source_target_pairs={{0,16},{1,17},{2,18},{3,19},{4,20},{5,21},{6,22},{7,23},{8,24},{9,... | collective-permute-start | bytes 24584 | tf_op jit(solution)/shard_map/ppermute | solution.py:17
  642.6 8.4 collective-permute-start.56
  704.0 9.2 %collective-permute-start.60 = (f32[2,1,8,128]{3,2,1,0:T(8,128)S(1)}, f32[2,1,8,128]{3,2,1,0:T(8,128)S(1)}, u32[]{:S(2)}, u32[]{:S(2)}) collective-permute-start(f32[2,1,8,128]{3,2,1,0:T(8,128)S(1)} %get-tuple-element.1145), channel_id=1, source_target_pairs={{0,16},{1,17},{2,18},{3,19},{4,20},{5,21},{6,22},{7,23},{8,24},{9,... | collective-permute-start | bytes 24584 | tf_op jit(solution)/shard_map/ppermute | solution.py:17
  721.5 6.2 collective-permute-start.64
  (53 other events, 218.2 us)
where the time goes:
time: 884 us; the launch traced here: 870 us
  blocking collectives  449 us (51%)
  starting transfers between devices  142 us (16%)
  waiting for transfers between devices  91.7 us (10%)
  between operations  81.8 us (9%)
  other arithmetic  49.5 us (6%)
  local copies, waits for them, and re-layouts  44.5 us (5%)
  matrix products  11.6 us (1%)
    psum x10, blocking collectives, body(): lax.psum((local_project, jnp.sum(applied * applied)), ('gx', 'gy', 'gz'))  407 us
    ppermute x33, starting transfers between devices, extended(): lax.ppermute(lax.slice_in_dim(block, block.shape[dim] - width, None, axis...  99.2 us
    ppermute x33, waiting for transfers between devices, extended(): lax.ppermute(lax.slice_in_dim(block, 0, width, axis=dim), axis, backward)  91.5 us
    ppermute x33, starting transfers between devices, extended(): lax.ppermute(lax.slice_in_dim(block, 0, width, axis=dim), axis, backward)  42.8 us
    psum x1, blocking collectives, body(): lax.psum(jnp.sum(source * source), ('gx', 'gy', 'gz'))  41.9 us
    another operation x26, other arithmetic  23.6 us
  transfers between devices with their start and end apart: 66, of which 31 were waited for; matrix products, arithmetic and copies ran while one was open for 5% of the time, Pallas kernels for 0%

commit v1 on v0

v1 whole, which is shorter than its diff:
```python
import functools
import math

import jax
import jax.numpy as jnp
from jax import lax
from jax.experimental import pallas as pl
from jax.experimental.pallas import tpu as pltpu
from jax.sharding import PartitionSpec as P

KRYLOV = 10
FIRST = 5
SCALE = 0.9
AXES = ("gx", "gy", "gz")
MESH = pl.DeviceIdType.MESH
highest = lax.Precision.HIGHEST

TAU = [math.cosh(k * math.acosh(1.0 / SCALE)) for k in range(KRYLOV + 1)]


def cholesky(matrix, count):
    lower = {}
    inverse_diag = []
    for j in range(count):
        pivot = matrix[j, j]
        for m in range(j):
            pivot = pivot - lower[j, m] * lower[j, m]
        inverse_root = lax.rsqrt(pivot)
        inverse_root = inverse_root * (1.5 - 0.5 * pivot * inverse_root * inverse_root)
        inverse_diag.append(inverse_root)
        for i in range(j + 1, count):
            value = matrix[i, j]
            for m in range(j):
                value = value - lower[i, m] * lower[j, m]
            lower[i, j] = value * inverse_root
    return lower, inverse_diag


def forward_solve(lower, inverse_diag, rhs):
    out = []
    for i in range(len(rhs)):
        value = rhs[i]
        for m in range(i):
            value = value - lower[i, m] * out[m]
        out.append(value * inverse_diag[i])
    return out


def backward_solve(lower, inverse_diag, rhs):
    count = len(rhs)
    out = [None] * count
    for i in range(count - 1, -1, -1):
        value = rhs[i]
        for m in range(i + 1, count):
            value = value - lower[m, i] * out[m]
        out[i] = value * inverse_diag[i]
    return out


def kernel(
    sizes,
    source,
    intra,
    extra,
    membrane,
    solution_ref,
    residual_ref,
    basis,
    faces_x,
    faces_y,
    faces_z,
    inverse,
    field,
    pack_y,
    pack_z,
    halo_x,
    halo_y,
    halo_z,
    gram,
    parts,
    send_sem,
    recv_sem,
    sum_send,
    sum_recv,
):
    planes, rows, lanes = source.shape[1:]
    total = 2 * planes
    place = [lax.axis_index(axis) for axis in AXES]
    lane = lax.broadcasted_iota(jnp.int32, (rows, lanes), 1)
    row = lax.broadcasted_iota(jnp.int32, (rows, lanes), 0)

    def edge_conditions(dim):
        return (place[dim] > 0, place[dim] < sizes[dim] - 1)

    halos = (halo_x, halo_y, halo_z)

    def send_source(dim, slot, side):
        if dim == 0:
            return field.at[slot, :, planes - 1 if side == 1 else 0]
        if dim == 1:
            return pack_y.at[slot, side]
        return pack_z.at[slot]

    def copy_to(dim, slot, side):
        return pltpu.make_async_remote_copy(
            src_ref=send_source(dim, slot, side),
            dst_ref=halos[dim].at[slot, 1 - side],
            send_sem=send_sem.at[slot, dim, side],
            recv_sem=recv_sem.at[slot, dim, 1 - side],
            device_id={AXES[dim]: place[dim] + (1 if side == 1 else -1)},
            device_id_type=MESH,
        )

    def copy_from(dim, slot, side):
        return pltpu.make_async_remote_copy(
            src_ref=send_source(dim, slot, side),
            dst_ref=halos[dim].at[slot, side],
            send_sem=send_sem.at[slot, dim, side],
            recv_sem=recv_sem.at[slot, dim, side],
            device_id={AXES[dim]: place[dim] + (1 if side == 1 else -1)},
            device_id_type=MESH,
        )

    def each_neighbour(action):
        for dim in (2, 1, 0):
            for side in range(2):
                pl.when(edge_conditions(dim)[side])(functools.partial(action, dim, side))

    def start(slot):
        each_neighbour(lambda dim, side: copy_to(dim, slot, side).start())

    def finish(slot):
        each_neighbour(lambda dim, side: copy_from(dim, slot, side).wait_recv())

    def drain(slot):
        each_neighbour(lambda dim, side: copy_to(dim, slot, side).wait_send())

    def set_packs(slot, values_y, values_z):
        pack_y[slot, 0] = jnp.concatenate([v[0:1] for v in values_y], axis=0)
        pack_y[slot, 1] = jnp.concatenate([v[rows - 1 : rows] for v in values_y], axis=0)
        edges = jnp.zeros((rows, lanes), jnp.float32)
        for k, value in enumerate(values_z):
            turned = pltpu.roll(value, 2 * k + 1, 1)
            edges = jnp.where((lane == 2 * k) | (lane == 2 * k + 1), turned, edges)
        pack_z[slot] = edges

    def zero_edges(dim, side):
        halos[dim][:, side] = jnp.zeros(halos[dim].shape[:1] + halos[dim].shape[2:], jnp.float32)

    for dim in range(3):
        for side in range(2):
            outside = place[dim] == (0 if side == 0 else sizes[dim] - 1)
            pl.when(outside)(functools.partial(zero_edges, dim, side))

    def halo_up_z(slot, k):
        return pltpu.roll(halo_z[slot, 1], lanes - 2 - 2 * k, 1)

    def halo_down_z(slot, k):
        return pltpu.roll(halo_z[slot, 0], (lanes - 2 * k) % lanes, 1)

    def halo_y_row(slot, side, k):
        return jnp.broadcast_to(halo_y[slot, side, k : k + 1, :], (rows, lanes))

    sigma = (intra, extra)
    for c in range(2):
        for x in (0, planes - 1):
            field[0, c, x] = sigma[c][0, x]
    order = [(c, x) for c in range(2) for x in range(planes)]
    set_packs(0, [sigma[c][1, x] for c, x in order], [sigma[c][2, x] for c, x in order])
    start(0)
    gram[...] = jnp.zeros_like(gram)
    for k, (c, x) in enumerate(order):
        basis[0, k] = source[c, x]
    finish(0)
    factor = 1.0 / SCALE
    diagonals = []
    for k, (c, x) in enumerate(order):
        mine = sigma[c][0, x]
        above = sigma[c][0, x + 1] if x < planes - 1 else halo_x[0, 1, c]
        below = sigma[c][0, x - 1] if x > 0 else halo_x[0, 0, c]
        up, down = mine + above, mine + below
        diagonal = up + down
        faces_x[0, k] = factor * up
        faces_x[1, k] = factor * down
        mine = sigma[c][1, x]
        above = jnp.where(row < rows - 1, pltpu.roll(mine, rows - 1, 0), halo_y_row(0, 1, k))
        below = jnp.where(row > 0, pltpu.roll(mine, 1, 0), halo_y_row(0, 0, k))
        up, down = mine + above, mine + below
        diagonal = diagonal + up + down
        up, down = factor * up, factor * down
        faces_y[0, k] = jnp.where(row < rows - 1, up, 0.0)
        faces_y[1, k] = jnp.where(row > 0, down, 0.0)
        faces_y[2, k] = jnp.where(row < rows - 1, 0.0, up)
        faces_y[3, k] = jnp.where(row > 0, 0.0, down)
        mine = sigma[c][2, x]
        above = jnp.where(lane < lanes - 1, pltpu.roll(mine, lanes - 1, 1), halo_up_z(0, k))
        below = jnp.where(lane > 0, pltpu.roll(mine, 1, 1), halo_down_z(0, k))
        up, down = mine + above, mine + below
        diagonal = diagonal + up + down
        up, down = factor * up, factor * down
        faces_z[0, k] = jnp.where(lane < lanes - 1, up, 0.0)
        faces_z[1, k] = jnp.where(lane > 0, down, 0.0)
        faces_z[2, k] = jnp.where(lane < lanes - 1, 0.0, up)
        faces_z[3, k] = jnp.where(lane > 0, 0.0, down)
        diagonals.append(0.5 * diagonal)
    for x in range(planes):
        di, de, m = diagonals[x], diagonals[planes + x], membrane[x]
        determinant = m * di + m * de + di * de
        inverse[0, x] = (di + de) / determinant
        inverse[1, x] = -di / determinant
        inverse[2, x] = (m + di) / determinant
    drain(0)

    def dots(new, others, first_row):
        for offset, other in enumerate(others):
            product = basis[new, 0] * basis[other, 0]
            for k in range(1, total):
                product = product + basis[new, k] * basis[other, k]
            gram[first_row + offset : first_row + offset + 1, :] = jnp.sum(
                product, axis=0, keepdims=True
            )

    def advance(index, restart, between):
        slot = (index + 1) % 2
        values = [None] * total
        for x in range(planes):
            first, second = basis[index, x], basis[index, planes + x]
            v = inverse[0, x] * first + inverse[1, x] * second
            p = inverse[1, x] * first + inverse[2, x] * second
            values[x], values[planes + x] = v + p, p
            field[slot, 0, x] = v + p
            field[slot, 1, x] = p
        set_packs(slot, values, values)
        start(slot)
        sums = []
        for k, (c, x) in enumerate(order):
            value = values[k]
            part = faces_y[0, k] * pltpu.roll(value, rows - 1, 0)
            part = part + faces_y[1, k] * pltpu.roll(value, 1, 0)
            part = part + faces_z[0, k] * pltpu.roll(value, lanes - 1, 1)
            part = part + faces_z[1, k] * pltpu.roll(value, 1, 1)
            if x < planes - 1:
                part = part + faces_x[0, k] * values[k + 1]
            if x > 0:
                part = part + faces_x[1, k] * values[k - 1]
            sums.append(part)
        between()
        finish(slot)
        for k, (c, x) in enumerate(order):
            part = sums[k]
            if x == planes - 1:
                part = part + faces_x[0, k] * halo_x[slot, 1, c]
            if x == 0:
                part = part + faces_x[1, k] * halo_x[slot, 0, c]
            part = part + faces_y[2, k] * halo_y_row(slot, 1, k)
            part = part + faces_y[3, k] * halo_y_row(slot, 0, k)
            part = part + faces_z[2, k] * halo_up_z(slot, k)
            part = part + faces_z[3, k] * halo_down_z(slot, k)
            sums[k] = part
        for x in range(planes):
            first, second = sums[x], sums[x] + sums[planes + x]
            if restart:
                basis[index + 1, x] = 0.5 * first
                basis[index + 1, planes + x] = 0.5 * second
            else:
                basis[index + 1, x] = first - basis[index - 1, x]
                basis[index + 1, planes + x] = second - basis[index - 1, planes + x]
        drain(slot)

    nx, ny, nz = sizes
    devices = nx * ny * nz
    me = (place[0] * ny + place[1]) * nz + place[2]

    def sum_copy(which, target):
        return pltpu.make_async_remote_copy(
            src_ref=parts.at[which, pl.ds(me, 1)],
            dst_ref=parts.at[which, pl.ds(me, 1)],
            send_sem=sum_send.at[which],
            recv_sem=sum_recv.at[which],
            device_id=target,
            device_id_type=MESH,
        )

    def reduced(which):
        ones = jnp.ones((8, lanes), jnp.float32)
        local = lax.dot_general(
            ones, gram[...], (((1,), (1,)), ((), ())), precision=highest,
            preferred_element_type=jnp.float32,
        )
        parts[which, pl.ds(me, 1), :] = local[0:1]
        if devices <= 64:
            for number in range(1, devices):
                dx, dy, dz = number // (ny * nz), number // nz % ny, number % nz
                target = tuple(
                    (place[d] + step) % sizes[d] if step else place[d]
                    for d, step in enumerate((dx, dy, dz))
                )
                sum_copy(which, target).start()
        else:

            def send(number, carry):
                other = (me + number) % devices
                sum_copy(which, (other // (ny * nz), other // nz % ny, other % nz)).start()
                return carry

            lax.fori_loop(1, devices, send, 0)
        everything = pltpu.make_async_remote_copy(
            src_ref=parts.at[which, pl.ds(0, devices - 1)],
            dst_ref=parts.at[which, pl.ds(0, devices - 1)],
            send_sem=sum_send.at[which],
            recv_sem=sum_recv.at[which],
            device_id=((place[0] + 1) % nx, place[1], place[2]),
            device_id_type=MESH,
        )
        everything.wait_recv()
        everything.wait_send()
        summed = jnp.broadcast_to(
            jnp.sum(parts[which], axis=0, keepdims=True), (rows, lanes)
        )

        def entry(number):
            return jnp.broadcast_to(summed[:, number : number + 1], (rows, lanes))

        return entry

    def triangle(j):
        return j * (j + 1) // 2

    for j in range(FIRST):
        advance(j, j == 0, lambda j=j: dots(j, range(j + 1), triangle(j)))
    dots(FIRST, range(FIRST), triangle(FIRST))
    entry = reduced(0)
    matrix = {}
    for j in range(FIRST):
        for i in range(j, FIRST):
            matrix[i, j] = entry(triangle(i) + j)
    factors = cholesky(matrix, FIRST)
    rhs = [entry(triangle(FIRST) + i) for i in range(FIRST)]
    shares = backward_solve(*factors, forward_solve(*factors, rhs))
    at_one = [jnp.full((rows, lanes), TAU[k], jnp.float32) for k in range(FIRST + 1)]
    for i in range(FIRST):
        at_one[FIRST] = at_one[FIRST] - shares[i] * TAU[i]
    for k in range(total):
        value = basis[FIRST, k]
        for i in range(FIRST):
            value = value - shares[i] * basis[i, k]
        basis[FIRST, k] = value

    for j in range(FIRST, KRYLOV):
        advance(j, j == FIRST, lambda j=j: dots(j, range(j + 1), triangle(j)))
        at_one.append(at_one[FIRST] * TAU[j + 1 - FIRST])
    dots(KRYLOV, range(KRYLOV + 1), triangle(KRYLOV))
    entry = reduced(1)
    matrix = {}
    for i in range(KRYLOV + 1):
        for j in range(i + 1):
            matrix[i, j] = entry(triangle(i) + j)
    factors = cholesky(matrix, KRYLOV + 1)
    half = forward_solve(*factors, at_one)
    length = half[0] * half[0]
    for value in half[1:]:
        length = length + value * value
    weights = backward_solve(*factors, [value / length for value in half])

    z = [None] * (KRYLOV + 2)
    z[KRYLOV] = z[KRYLOV + 1] = jnp.zeros((rows, lanes), jnp.float32)
    for i in range(KRYLOV, 0, -1):
        value = weights[i] + (z[i] if i < KRYLOV else 0.0)
        above = z[i + 1] if i + 1 < KRYLOV and i != FIRST - 1 else None
        if i < FIRST:
            extra_term = shares[i] * z[FIRST - 1]
            above = extra_term if above is None else above + extra_term
        if i in (1, FIRST + 1):
            value = value * (1.0 / SCALE)
            above = None if above is None else 0.5 * above
        else:
            value = value * (2.0 / SCALE)
        z[i - 1] = value if above is None else value - above

    for x in range(planes):
        first = z[0] * basis[0, x]
        second = z[0] * basis[0, planes + x]
        for j in range(1, KRYLOV):
            first = first + z[j] * basis[j, x]
            second = second + z[j] * basis[j, planes + x]
        solution_ref[0, x] = inverse[0, x] * first + inverse[1, x] * second
        solution_ref[1, x] = inverse[1, x] * first + inverse[2, x] * second
    for k, (c, x) in enumerate(order):
        value = weights[0] * basis[0, k]
        for j in range(1, KRYLOV + 1):
            value = value + weights[j] * basis[j, k]
        residual_ref[c, x] = value


def solution(mesh):
    sizes = tuple(mesh.shape[axis] for axis in AXES)
    devices = sizes[0] * sizes[1] * sizes[2]

    def body(source, sigma_intra, sigma_extra, membrane):
        planes, rows, lanes = membrane.shape
        total = 2 * planes
        f32 = jnp.float32
        vmem = pl.BlockSpec(memory_space=pltpu.VMEM)
        return pl.pallas_call(
            functools.partial(kernel, sizes),
            out_shape=(jax.ShapeDtypeStruct(source.shape, f32),) * 2,
            in_specs=[vmem] * 4,
            out_specs=(vmem, vmem),
            scratch_shapes=[
                pltpu.VMEM((KRYLOV + 1, total, rows, lanes), f32),
                pltpu.VMEM((2, total, rows, lanes), f32),
                pltpu.VMEM((4, total, rows, lanes), f32),
                pltpu.VMEM((4, total, rows, lanes), f32),
                pltpu.VMEM((3, planes, rows, lanes), f32),
                pltpu.VMEM((2, 2, planes, rows, lanes), f32),
                pltpu.VMEM((2, 2, total, lanes), f32),
                pltpu.VMEM((2, rows, lanes), f32),
                pltpu.VMEM((2, 2, 2, rows, lanes), f32),
                pltpu.VMEM((2, 2, total, lanes), f32),
                pltpu.VMEM((2, 2, rows, lanes), f32),
                pltpu.VMEM((128, lanes), f32),
                pltpu.VMEM((2, devices, 128), f32),
                pltpu.SemaphoreType.DMA((2, 3, 2)),
                pltpu.SemaphoreType.DMA((2, 3, 2)),
                pltpu.SemaphoreType.DMA((2,)),
                pltpu.SemaphoreType.DMA((2,)),
            ],
            compiler_params=pltpu.CompilerParams(has_side_effects=True),
        )(source, sigma_intra, sigma_extra, membrane)

    spec = P(None, "gx", "gy", "gz")
    return jax.shard_map(
        body,
        mesh=mesh,
        in_specs=(spec, spec, spec, P("gx", "gy", "gz")),
        out_specs=(spec, spec),
        check_vma=False,
    )
```

time: 884 us -> 54.7 us (0.06); the launches traced: 870 us -> 54.5 us
  blocking collectives: 449 us -> 0 us
  starting transfers between devices: 142 us -> 0 us
  waiting for transfers between devices: 91.7 us -> 0 us
  between operations: 81.8 us -> 0.65 us
  Pallas kernels: 0 us -> 51.8 us
  other arithmetic: 49.5 us -> 0 us
  local copies, waits for them, and re-layouts: 44.5 us -> 2 us
  matrix products: 11.6 us -> 0 us
    psum x11 -> x0, blocking collectives: 449 us -> none  [the longest x10 407 us: body(): lax.psum((local_project, jnp.sum(applied * applied)), ('gx', 'gy', 'gz'))]
    ppermute x66 -> x0, starting transfers between devices: 142 us -> none  [the longest x33 99.2 us: extended(): lax.ppermute(lax.slice_in_dim(block, block.shape[dim] - width, None, axis...]
    ppermute x66 -> x0, waiting for transfers between devices: 91.7 us -> none  [the longest x33 91.5 us: extended(): lax.ppermute(lax.slice_in_dim(block, 0, width, axis=dim), axis, backward)]
    pallas_call x0 -> x1, Pallas kernels: none -> 51.8 us  [body(): pl.pallas_call(functools.partial(kernel, sizes), out_shape=(jax.ShapeDtyp...]
    another operation x58 -> x0, other arithmetic: 26.3 us -> none
    slice x57 -> x0, local copies, waits for them, and re-layouts: 18.2 us -> none  [the longest x10 5.59 us: least_squares(): pivot = rotated[column, column]]
    reduce_sum x27 -> x0, other arithmetic: 17.9 us -> none  [the longest x8 5.9 us: least_squares(): partial_sum = jnp.sum(rotated[column, column + 1:] * coeffs[column + 1:])]
    scatter x58 -> x0, local copies, waits for them, and re-layouts: 17.1 us -> none  [the longest x20 15.3 us: body(): hessenberg.at[:column + 1, column].set(project).at[column + 1, column]]
  transfers between devices with their start and end apart: 66 -> 0, of which waited for: 31 -> 0; matrix products, arithmetic and copies ran while one was open for 5% -> 0% of each run, Pallas kernels for 0% -> 0%
where the time goes in v1:
time: 54.7 us; the launch traced here: 54.5 us
  Pallas kernels  51.8 us (95%)
  local copies, waits for them, and re-layouts  2 us (4%)
  between operations  0.65 us (1%)
    pallas_call x1, Pallas kernels, body(): pl.pallas_call(functools.partial(kernel, sizes), out_shape=(jax.ShapeDtyp...  51.8 us
    unnamed x4, local copies, waits for them, and re-layouts  2 us

profile of v1, /device:TPU:0, one launch (start us, length us, event | category | flops | bytes accessed | tf_op | source)
XLA Modules:
  0.0 54.5 jit_solution(10910591276580305301)
XLA Ops:
  0.6 51.8 %shard_map.59 = (f32[2,4,8,128]{3,2,1,0:T(8,128)}, f32[2,4,8,128]{3,2,1,0:T(8,128)}) custom-call(f32[2,4,8,128]{3,2,1,0:T(8,128)} %source.1, f32[3,4,8,128]{3,2,1,0:T(8,128)} %intra.1, f32[3,4,8,128]{3,2,1,0:T(8,128)} %extra.1, f32[4,8,128]{2,1,0:T(8,128)} %membrane.1), custom_call_target="tpu_custom_call" | custom-call | tf_op jit(solution)/shard_map/pallas_call | solution.py:404
  52.4 0.0 copy-start
  52.5 1.4 %copy.8 = f32[2,4,8,128]{3,2,1,0:T(8,128)} copy(f32[2,4,8,128]{3,2,1,0:T(8,128)} %get-tuple-element.4) | data formatting | bytes 65536
  53.8 0.0 copy-done
  53.8 0.6 %copy.9 = f32[2,4,8,128]{3,2,1,0:T(8,128)} copy(f32[2,4,8,128]{3,2,1,0:T(8,128)S(1)} %copy-done) | data formatting | bytes 65536
Async XLA Ops:
  52.4 1.4 %copy-start = (f32[2,4,8,128]{3,2,1,0:T(8,128)S(1)}, f32[2,4,8,128]{3,2,1,0:T(8,128)}, u32[]{:S(2)}) copy-start(f32[2,4,8,128]{3,2,1,0:T(8,128)} %get-tuple-element.5) | copy-start | bytes 98308

commit v2 on v1

--- a/solution.py
+++ b/solution.py
@@ -1,5 +1,4 @@
 import functools
-import math
 
 import jax
 import jax.numpy as jnp
@@ -10,12 +9,11 @@
 
 KRYLOV = 10
 FIRST = 5
-SCALE = 0.9
+LAG = 3
+ORTHO = FIRST + LAG + 1
 AXES = ("gx", "gy", "gz")
 MESH = pl.DeviceIdType.MESH
 highest = lax.Precision.HIGHEST
-
-TAU = [math.cosh(k * math.acosh(1.0 / SCALE)) for k in range(KRYLOV + 1)]
 
 
 def cholesky(matrix, count):
@@ -86,6 +84,9 @@
     planes, rows, lanes = source.shape[1:]
     total = 2 * planes
     place = [lax.axis_index(axis) for axis in AXES]
+    nx, ny, nz = sizes
+    devices = nx * ny * nz
+    me = (place[0] * ny + place[1]) * nz + place[2]
     lane = lax.broadcasted_iota(jnp.int32, (rows, lanes), 1)
     row = lax.broadcasted_iota(jnp.int32, (rows, lanes), 0)
 
@@ -160,6 +161,37 @@
 
     def halo_y_row(slot, side, k):
         return jnp.broadcast_to(halo_y[slot, side, k : k + 1, :], (rows, lanes))
+
+    barrier = pltpu.get_barrier_semaphore()
+    if sum(sizes) - 3 <= FIRST + 2:
+        def greet(dim, side):
+            pl.semaphore_signal(
+                barrier,
+                inc=1,
+                device_id={AXES[dim]: place[dim] + (1 if side == 1 else -1)},
+                device_id_type=MESH,
+            )
+
+        each_neighbour(greet)
+        expected = 0
+        for dim in range(3):
+            for side in range(2):
+                expected = expected + edge_conditions(dim)[side].astype(jnp.int32)
+        pl.semaphore_wait(barrier, expected)
+    else:
+
+        def greet_all(number, carry):
+            other = (me + number) % devices
+            pl.semaphore_signal(
+                barrier,
+                inc=1,
+                device_id=(other // (ny * nz), other // nz % ny, other % nz),
+                device_id_type=MESH,
+            )
+            return carry
+
+        lax.fori_loop(1, devices, greet_all, 0)
+        pl.semaphore_wait(barrier, devices - 1)
 
     sigma = (intra, extra)
     for c in range(2):
@@ -172,7 +204,6 @@
     for k, (c, x) in enumerate(order):
         basis[0, k] = source[c, x]
     finish(0)
-    factor = 1.0 / SCALE
     diagonals = []
     for k, (c, x) in enumerate(order):
         mine = sigma[c][0, x]
@@ -180,14 +211,13 @@
         below = sigma[c][0, x - 1] if x > 0 else halo_x[0, 0, c]
         up, down = mine + above, mine + below
         diagonal = up + down
-        faces_x[0, k] = factor * up
-        faces_x[1, k] = factor * down
+        faces_x[0, k] = up
+        faces_x[1, k] = down
         mine = sigma[c][1, x]
         above = jnp.where(row < rows - 1, pltpu.roll(mine, rows - 1, 0), halo_y_row(0, 1, k))
         below = jnp.where(row > 0, pltpu.roll(mine, 1, 0), halo_y_row(0, 0, k))
         up, down = mine + above, mine + below
         diagonal = diagonal + up + down
-        up, down = factor * up, factor * down
         faces_y[0, k] = jnp.where(row < rows - 1, up, 0.0)
         faces_y[1, k] = jnp.where(row > 0, down, 0.0)
         faces_y[2, k] = jnp.where(row < rows - 1, 0.0, up)
@@ -197,7 +227,6 @@
         below = jnp.where(lane > 0, pltpu.roll(mine, 1, 1), halo_down_z(0, k))
         up, down = mine + above, mine + below
         diagonal = diagonal + up + down
-        up, down = factor * up, factor * down
         faces_z[0, k] = jnp.where(lane < lanes - 1, up, 0.0)
         faces_z[1, k] = jnp.where(lane > 0, down, 0.0)
         faces_z[2, k] = jnp.where(lane < lanes - 1, 0.0, up)
@@ -220,8 +249,7 @@
                 product, axis=0, keepdims=True
             )
 
-    def advance(index, restart, between):
-        slot = (index + 1) % 2
+    def advance(slot, index, restart, between):
         values = [None] * total
         for x in range(planes):
             first, second = basis[index, x], basis[index, planes + x]
@@ -267,10 +295,6 @@
                 basis[index + 1, planes + x] = second - basis[index - 1, planes + x]
         drain(slot)
 
-    nx, ny, nz = sizes
-    devices = nx * ny * nz
-    me = (place[0] * ny + place[1]) * nz + place[2]
-
     def sum_copy(which, target):
         return pltpu.make_async_remote_copy(
             src_ref=parts.at[which, pl.ds(me, 1)],
@@ -281,7 +305,7 @@
             device_id_type=MESH,
         )
 
-    def reduced(which):
+    def start_sum(which):
         ones = jnp.ones((8, lanes), jnp.float32)
         local = lax.dot_general(
             ones, gram[...], (((1,), (1,)), ((), ())), precision=highest,
@@ -304,6 +328,7 @@
                 return carry
 
             lax.fori_loop(1, devices, send, 0)
+    def finish_sum(which):
         everything = pltpu.make_async_remote_copy(
             src_ref=parts.at[which, pl.ds(0, devices - 1)],
             dst_ref=parts.at[which, pl.ds(0, devices - 1)],
@@ -327,68 +352,104 @@
         return j * (j + 1) // 2
 
     for j in range(FIRST):
-        advance(j, j == 0, lambda j=j: dots(j, range(j + 1), triangle(j)))
+        advance((j + 1) % 2, j, j == 0, lambda j=j: dots(j, range(j + 1), triangle(j)))
     dots(FIRST, range(FIRST), triangle(FIRST))
-    entry = reduced(0)
-    matrix = {}
-    for j in range(FIRST):
-        for i in range(j, FIRST):
-            matrix[i, j] = entry(triangle(i) + j)
-    factors = cholesky(matrix, FIRST)
-    rhs = [entry(triangle(FIRST) + i) for i in range(FIRST)]
-    shares = backward_solve(*factors, forward_solve(*factors, rhs))
-    at_one = [jnp.full((rows, lanes), TAU[k], jnp.float32) for k in range(FIRST + 1)]
-    for i in range(FIRST):
-        at_one[FIRST] = at_one[FIRST] - shares[i] * TAU[i]
+    start_sum(0)
+    found = {}
+
+    def orthonormalise():
+        entry = finish_sum(0)
+        matrix = {}
+        for j in range(FIRST):
+            for i in range(j, FIRST):
+                matrix[i, j] = entry(triangle(i) + j)
+        factors = cholesky(matrix, FIRST)
+        on_ortho = forward_solve(*factors, [entry(triangle(FIRST) + i) for i in range(FIRST)])
+        shares = backward_solve(*factors, on_ortho)
+        at_one = forward_solve(*factors, [jnp.ones((rows, lanes), jnp.float32)] * FIRST)
+        last = 1.0 - on_ortho[0] * at_one[0]
+        for i in range(1, FIRST):
+            last = last - on_ortho[i] * at_one[i]
+        found.update(
+            factors=factors, shares=shares, at_one=at_one + [last] * (KRYLOV + 1 - FIRST)
+        )
+        lower, inverse_diag = factors
+        for k in range(total):
+            made = []
+            for i in range(FIRST):
+                value = basis[i, k]
+                for m in range(i):
+                    value = value - lower[i, m] * made[m]
+                value = value * inverse_diag[i]
+                made.append(value)
+                basis[ORTHO + i, k] = value
+        for i in range(FIRST):
+            dots(ORTHO + i, range(ORTHO, ORTHO + i + 1), triangle(i))
+
+    for j in range(FIRST, FIRST + LAG):
+        advance(
+            (j + 1) % 2, j, False, orthonormalise if j == FIRST + LAG - 1 else lambda: None
+        )
+    shares = found["shares"]
+
+    middle = ORTHO + FIRST
     for k in range(total):
         value = basis[FIRST, k]
         for i in range(FIRST):
             value = value - shares[i] * basis[i, k]
-        basis[FIRST, k] = value
-
-    for j in range(FIRST, KRYLOV):
-        advance(j, j == FIRST, lambda j=j: dots(j, range(j + 1), triangle(j)))
-        at_one.append(at_one[FIRST] * TAU[j + 1 - FIRST])
-    dots(KRYLOV, range(KRYLOV + 1), triangle(KRYLOV))
-    entry = reduced(1)
+        basis[middle, k] = value
+        for m in range(1, LAG + 1):
+            value = basis[FIRST + m, k] + basis[abs(FIRST - m), k]
+            for i in range(FIRST):
+                value = value - shares[i] * (basis[i + m, k] + basis[abs(i - m), k])
+            basis[middle + m, k] = 0.5 * value
+    for j in range(FIRST + LAG, KRYLOV):
+
+        def between(j=j):
+            for i in range(FIRST if j == FIRST + LAG else j, j + 1):
+                dots(ORTHO + i, range(ORTHO, ORTHO + i + 1), triangle(i))
+
+        advance((j + 1) % 2, ORTHO + j, False, between)
+    dots(ORTHO + KRYLOV, range(ORTHO, ORTHO + KRYLOV + 1), triangle(KRYLOV))
+    start_sum(1)
+    entry = finish_sum(1)
     matrix = {}
     for i in range(KRYLOV + 1):
         for j in range(i + 1):
             matrix[i, j] = entry(triangle(i) + j)
     factors = cholesky(matrix, KRYLOV + 1)
-    half = forward_solve(*factors, at_one)
+    half = forward_solve(*factors, found["at_one"])
     length = half[0] * half[0]
     for value in half[1:]:
         length = length + value * value
     weights = backward_solve(*factors, [value / length for value in half])
 
-    z = [None] * (KRYLOV + 2)
-    z[KRYLOV] = z[KRYLOV + 1] = jnp.zeros((rows, lanes), jnp.float32)
+    target = backward_solve(*found["factors"], weights[:FIRST]) + weights[FIRST:]
+    z = [None] * KRYLOV
     for i in range(KRYLOV, 0, -1):
-        value = weights[i] + (z[i] if i < KRYLOV else 0.0)
+        value = target[i] + z[i] if i < KRYLOV else target[i]
         above = z[i + 1] if i + 1 < KRYLOV and i != FIRST - 1 else None
         if i < FIRST:
-            extra_term = shares[i] * z[FIRST - 1]
-            above = extra_term if above is None else above + extra_term
+            share = shares[i] * z[FIRST - 1]
+            above = share if above is None else above + share
         if i in (1, FIRST + 1):
-            value = value * (1.0 / SCALE)
-            above = None if above is None else 0.5 * above
+            z[i - 1] = value - 0.5 * above
         else:
-            value = value * (2.0 / SCALE)
-        z[i - 1] = value if above is None else value - above
+            z[i - 1] = 2.0 * value if above is None else 2.0 * value - above
 
     for x in range(planes):
         first = z[0] * basis[0, x]
         second = z[0] * basis[0, planes + x]
         for j in range(1, KRYLOV):
-            first = first + z[j] * basis[j, x]
-            second = second + z[j] * basis[j, planes + x]
+            at = j if j < FIRST else ORTHO + j
+            first = first + z[j] * basis[at, x]
+            second = second + z[j] * basis[at, planes + x]
         solution_ref[0, x] = inverse[0, x] * first + inverse[1, x] * second
         solution_ref[1, x] = inverse[1, x] * first + inverse[2, x] * second
     for k, (c, x) in enumerate(order):
-        value = weights[0] * basis[0, k]
+        value = weights[0] * basis[ORTHO, k]
         for j in range(1, KRYLOV + 1):
-            value = value + weights[j] * basis[j, k]
+            value = value + weights[j] * basis[ORTHO + j, k]
         residual_ref[c, x] = value
 
 
@@ -407,7 +468,7 @@
             in_specs=[vmem] * 4,
             out_specs=(vmem, vmem),
             scratch_shapes=[
-                pltpu.VMEM((KRYLOV + 1, total, rows, lanes), f32),
+                pltpu.VMEM((ORTHO + KRYLOV + 1, total, rows, lanes), f32),
                 pltpu.VMEM((2, total, rows, lanes), f32),
                 pltpu.VMEM((4, total, rows, lanes), f32),
                 pltpu.VMEM((4, total, rows, lanes), f32),
@@ -425,7 +486,7 @@
                 pltpu.SemaphoreType.DMA((2,)),
                 pltpu.SemaphoreType.DMA((2,)),
             ],
-            compiler_params=pltpu.CompilerParams(has_side_effects=True),
+            compiler_params=pltpu.CompilerParams(collective_id=0, has_side_effects=True),
         )(source, sigma_intra, sigma_extra, membrane)
 
     spec = P(None, "gx", "gy", "gz")

time: 54.7 us -> 46.4 us (0.85)
  Pallas kernels: 51.8 us -> 43.5 us
    pallas_call x1, Pallas kernels: 51.8 us -> 43.5 us  [body(): pl.pallas_call(functools.partial(kernel, sizes), out_shape=(jax.ShapeDtyp...]
where the time goes in v2:
time: 46.4 us; the launch traced here: 46.1 us
  Pallas kernels  43.5 us (94%)
  local copies, waits for them, and re-layouts  2 us (4%)
  between operations  0.65 us (1%)
    pallas_call x1, Pallas kernels, body(): pl.pallas_call(functools.partial(kernel, sizes), out_shape=(jax.ShapeDtyp...  43.5 us
    unnamed x4, local copies, waits for them, and re-layouts  2 us

profile of v2, /device:TPU:0, one launch (start us, length us, event | category | flops | bytes accessed | tf_op | source)
XLA Modules:
  0.0 46.1 jit_solution(1495093819518963140)
XLA Ops:
  0.6 43.5 %shard_map.59 = (f32[2,4,8,128]{3,2,1,0:T(8,128)}, f32[2,4,8,128]{3,2,1,0:T(8,128)}) custom-call(f32[2,4,8,128]{3,2,1,0:T(8,128)} %source.1, f32[3,4,8,128]{3,2,1,0:T(8,128)} %intra.1, f32[3,4,8,128]{3,2,1,0:T(8,128)} %extra.1, f32[4,8,128]{2,1,0:T(8,128)} %membrane.1), custom_call_target="tpu_custom_call" | custom-call | tf_op jit(solution)/shard_map/pallas_call | solution.py:465
  44.1 0.0 copy-start
  44.1 1.4 %copy.8 = f32[2,4,8,128]{3,2,1,0:T(8,128)} copy(f32[2,4,8,128]{3,2,1,0:T(8,128)} %get-tuple-element.4) | data formatting | bytes 65536
  45.5 0.0 copy-done
  45.5 0.6 %copy.9 = f32[2,4,8,128]{3,2,1,0:T(8,128)} copy(f32[2,4,8,128]{3,2,1,0:T(8,128)S(1)} %copy-done) | data formatting | bytes 65536
Async XLA Ops:
  44.1 1.4 %copy-start = (f32[2,4,8,128]{3,2,1,0:T(8,128)S(1)}, f32[2,4,8,128]{3,2,1,0:T(8,128)}, u32[]{:S(2)}) copy-start(f32[2,4,8,128]{3,2,1,0:T(8,128)} %get-tuple-element.5) | copy-start | bytes 98308

commit v3 on v2

--- a/solution.py
+++ b/solution.py
@@ -57,10 +57,10 @@
 
 def kernel(
     sizes,
-    source,
-    intra,
-    extra,
-    membrane,
+    source_hbm,
+    intra_hbm,
+    extra_hbm,
+    membrane_hbm,
     solution_ref,
     residual_ref,
     basis,
@@ -80,8 +80,12 @@
     recv_sem,
     sum_send,
     sum_recv,
+    intra,
+    extra,
+    membrane,
+    input_sem,
 ):
-    planes, rows, lanes = source.shape[1:]
+    planes, rows, lanes = membrane_hbm.shape
     total = 2 * planes
     place = [lax.axis_index(axis) for axis in AXES]
     nx, ny, nz = sizes
@@ -122,13 +126,13 @@
             device_id_type=MESH,
         )
 
-    def each_neighbour(action):
-        for dim in (2, 1, 0):
+    def each_neighbour(action, dims=(2, 1, 0)):
+        for dim in dims:
             for side in range(2):
                 pl.when(edge_conditions(dim)[side])(functools.partial(action, dim, side))
 
-    def start(slot):
-        each_neighbour(lambda dim, side: copy_to(dim, slot, side).start())
+    def start(slot, dims):
+        each_neighbour(lambda dim, side: copy_to(dim, slot, side).start(), dims)
 
     def finish(slot):
         each_neighbour(lambda dim, side: copy_from(dim, slot, side).wait_recv())
@@ -136,9 +140,11 @@
     def drain(slot):
         each_neighbour(lambda dim, side: copy_to(dim, slot, side).wait_send())
 
-    def set_packs(slot, values_y, values_z):
+    def set_pack_y(slot, values_y):
         pack_y[slot, 0] = jnp.concatenate([v[0:1] for v in values_y], axis=0)
         pack_y[slot, 1] = jnp.concatenate([v[rows - 1 : rows] for v in values_y], axis=0)
+
+    def set_pack_z(slot, values_z):
         edges = jnp.zeros((rows, lanes), jnp.float32)
         for k, value in enumerate(values_z):
             turned = pltpu.roll(value, 2 * k + 1, 1)
@@ -162,6 +168,14 @@
     def halo_y_row(slot, side, k):
         return jnp.broadcast_to(halo_y[slot, side, k : k + 1, :], (rows, lanes))
 
+    loads = [
+        pltpu.make_async_copy(intra_hbm, intra, input_sem.at[0]),
+        pltpu.make_async_copy(extra_hbm, extra, input_sem.at[1]),
+        pltpu.make_async_copy(membrane_hbm, membrane, input_sem.at[2]),
+        pltpu.make_async_copy(source_hbm, basis.at[0], input_sem.at[3]),
+    ]
+    for load in loads:
+        load.start()
     barrier = pltpu.get_barrier_semaphore()
     if sum(sizes) - 3 <= FIRST + 2:
         def greet(dim, side):
@@ -177,7 +191,6 @@
         for dim in range(3):
             for side in range(2):
                 expected = expected + edge_conditions(dim)[side].astype(jnp.int32)
-        pl.semaphore_wait(barrier, expected)
     else:
 
         def greet_all(number, carry):
@@ -191,18 +204,22 @@
             return carry
 
         lax.fori_loop(1, devices, greet_all, 0)
-        pl.semaphore_wait(barrier, devices - 1)
+        expected = devices - 1
 
     sigma = (intra, extra)
+    loads[0].wait()
+    loads[1].wait()
     for c in range(2):
         for x in (0, planes - 1):
             field[0, c, x] = sigma[c][0, x]
     order = [(c, x) for c in range(2) for x in range(planes)]
-    set_packs(0, [sigma[c][1, x] for c, x in order], [sigma[c][2, x] for c, x in order])
-    start(0)
+    set_pack_y(0, [sigma[c][1, x] for c, x in order])
+    set_pack_z(0, [sigma[c][2, x] for c, x in order])
+    pl.semaphore_wait(barrier, expected)
+    start(0, (0, 1, 2))
     gram[...] = jnp.zeros_like(gram)
-    for k, (c, x) in enumerate(order):
-        basis[0, k] = source[c, x]
+    loads[2].wait()
+    loads[3].wait()
     finish(0)
     diagonals = []
     for k, (c, x) in enumerate(order):
@@ -238,7 +255,6 @@
         inverse[0, x] = (di + de) / determinant
         inverse[1, x] = -di / determinant
         inverse[2, x] = (m + di) / determinant
-    drain(0)
 
     def dots(new, others, first_row):
         for offset, other in enumerate(others):
@@ -258,8 +274,11 @@
             values[x], values[planes + x] = v + p, p
             field[slot, 0, x] = v + p
             field[slot, 1, x] = p
-        set_packs(slot, values, values)
-        start(slot)
+        start(slot, (0,))
+        set_pack_y(slot, values)
+        start(slot, (1,))
+        set_pack_z(slot, values)
+        start(slot, (2,))
         sums = []
         for k, (c, x) in enumerate(order):
             value = values[k]
@@ -273,6 +292,7 @@
                 part = part + faces_x[1, k] * values[k - 1]
             sums.append(part)
         between()
+        drain(1 - slot)
         finish(slot)
         for k, (c, x) in enumerate(order):
             part = sums[k]
@@ -293,7 +313,6 @@
             else:
                 basis[index + 1, x] = first - basis[index - 1, x]
                 basis[index + 1, planes + x] = second - basis[index - 1, planes + x]
-        drain(slot)
 
     def sum_copy(which, target):
         return pltpu.make_async_remote_copy(
@@ -412,6 +431,7 @@
         advance((j + 1) % 2, ORTHO + j, False, between)
     dots(ORTHO + KRYLOV, range(ORTHO, ORTHO + KRYLOV + 1), triangle(KRYLOV))
     start_sum(1)
+    drain(KRYLOV % 2)
     entry = finish_sum(1)
     matrix = {}
     for i in range(KRYLOV + 1):
@@ -465,7 +485,7 @@
         return pl.pallas_call(
             functools.partial(kernel, sizes),
             out_shape=(jax.ShapeDtypeStruct(source.shape, f32),) * 2,
-            in_specs=[vmem] * 4,
+            in_specs=[pl.BlockSpec(memory_space=pl.ANY)] * 4,
             out_specs=(vmem, vmem),
             scratch_shapes=[
                 pltpu.VMEM((ORTHO + KRYLOV + 1, total, rows, lanes), f32),
@@ -485,9 +505,13 @@
                 pltpu.SemaphoreType.DMA((2, 3, 2)),
                 pltpu.SemaphoreType.DMA((2,)),
                 pltpu.SemaphoreType.DMA((2,)),
+                pltpu.VMEM(sigma_intra.shape, f32),
+                pltpu.VMEM(sigma_extra.shape, f32),
+                pltpu.VMEM(membrane.shape, f32),
+                pltpu.SemaphoreType.DMA((4,)),
             ],
             compiler_params=pltpu.CompilerParams(collective_id=0, has_side_effects=True),
-        )(source, sigma_intra, sigma_extra, membrane)
+        )(source.reshape(total, rows, lanes), sigma_intra, sigma_extra, membrane)
 
     spec = P(None, "gx", "gy", "gz")
     return jax.shard_map(

time: 46.4 us -> 44.7 us (0.963)
  Pallas kernels: 43.5 us -> 41.8 us
    pallas_call x1, Pallas kernels: 43.5 us -> 41.8 us  [body(): pl.pallas_call(functools.partial(kernel, sizes), out_shape=(jax.ShapeDtyp...]
where the time goes in v3:
time: 44.7 us; the launch traced here: 44.5 us
  Pallas kernels  41.8 us (94%)
  local copies, waits for them, and re-layouts  2 us (4%)
  between operations  0.65 us (1%)
    pallas_call x1, Pallas kernels, body(): pl.pallas_call(functools.partial(kernel, sizes), out_shape=(jax.ShapeDtyp...  41.8 us
    unnamed x4, local copies, waits for them, and re-layouts  2 us

profile of v3, /device:TPU:0, one launch (start us, length us, event | category | flops | bytes accessed | tf_op | source)
XLA Modules:
  0.0 44.5 jit_solution(17227963445276996684)
XLA Ops:
  0.6 41.8 %shard_map.59 = (f32[2,4,8,128]{3,2,1,0:T(8,128)}, f32[2,4,8,128]{3,2,1,0:T(8,128)}) custom-call(f32[8,8,128]{2,1,0:T(8,128)} %bitcast.1, f32[3,4,8,128]{3,2,1,0:T(8,128)} %intra_hbm.1, f32[3,4,8,128]{3,2,1,0:T(8,128)} %extra_hbm.1, f32[4,8,128]{2,1,0:T(8,128)} %membrane_hbm.1), custom_call_target="tpu_custom_call" | custom-call | tf_op jit(solution)/shard_map/pallas_call | solution.py:485
  42.5 0.0 copy-start
  42.5 1.4 %copy.8 = f32[2,4,8,128]{3,2,1,0:T(8,128)} copy(f32[2,4,8,128]{3,2,1,0:T(8,128)} %get-tuple-element.4) | data formatting | bytes 65536
  43.8 0.0 copy-done
  43.8 0.6 %copy.9 = f32[2,4,8,128]{3,2,1,0:T(8,128)} copy(f32[2,4,8,128]{3,2,1,0:T(8,128)S(1)} %copy-done) | data formatting | bytes 65536
Async XLA Ops:
  42.5 1.4 %copy-start = (f32[2,4,8,128]{3,2,1,0:T(8,128)S(1)}, f32[2,4,8,128]{3,2,1,0:T(8,128)}, u32[]{:S(2)}) copy-start(f32[2,4,8,128]{3,2,1,0:T(8,128)} %get-tuple-element.5) | copy-start | bytes 98308

commit v4 on v3

--- a/solution.py
+++ b/solution.py
@@ -134,8 +134,8 @@
     def start(slot, dims):
         each_neighbour(lambda dim, side: copy_to(dim, slot, side).start(), dims)
 
-    def finish(slot):
-        each_neighbour(lambda dim, side: copy_from(dim, slot, side).wait_recv())
+    def finish(slot, dims=(0, 1, 2)):
+        each_neighbour(lambda dim, side: copy_from(dim, slot, side).wait_recv(), dims)
 
     def drain(slot):
         each_neighbour(lambda dim, side: copy_to(dim, slot, side).wait_send())
@@ -293,7 +293,7 @@
             sums.append(part)
         between()
         drain(1 - slot)
-        finish(slot)
+        finish(slot, (0, 1))
         for k, (c, x) in enumerate(order):
             part = sums[k]
             if x == planes - 1:
@@ -302,9 +302,11 @@
                 part = part + faces_x[1, k] * halo_x[slot, 0, c]
             part = part + faces_y[2, k] * halo_y_row(slot, 1, k)
             part = part + faces_y[3, k] * halo_y_row(slot, 0, k)
-            part = part + faces_z[2, k] * halo_up_z(slot, k)
-            part = part + faces_z[3, k] * halo_down_z(slot, k)
             sums[k] = part
+        finish(slot, (2,))
+        for k in range(total):
+            part = sums[k] + faces_z[2, k] * halo_up_z(slot, k)
+            sums[k] = part + faces_z[3, k] * halo_down_z(slot, k)
         for x in range(planes):
             first, second = sums[x], sums[x] + sums[planes + x]
             if restart:
@@ -357,7 +359,7 @@
             device_id_type=MESH,
         )
         everything.wait_recv()
-        everything.wait_send()
+        pending.append(everything)
         summed = jnp.broadcast_to(
             jnp.sum(parts[which], axis=0, keepdims=True), (rows, lanes)
         )
@@ -375,6 +377,7 @@
     dots(FIRST, range(FIRST), triangle(FIRST))
     start_sum(0)
     found = {}
+    pending = []
 
     def orthonormalise():
         entry = finish_sum(0)
@@ -410,6 +413,7 @@
             (j + 1) % 2, j, False, orthonormalise if j == FIRST + LAG - 1 else lambda: None
         )
     shares = found["shares"]
+    pending.pop().wait_send()
 
     middle = ORTHO + FIRST
     for k in range(total):
@@ -471,6 +475,7 @@
         for j in range(1, KRYLOV + 1):
             value = value + weights[j] * basis[ORTHO + j, k]
         residual_ref[c, x] = value
+    pending.pop().wait_send()
 
 
 def solution(mesh):

time: 44.7 us -> 44.9 us (level)
  no operation moved by 1% of the time
where the time goes in v4:
time: 44.9 us; the launch traced here: 44.7 us
  Pallas kernels  42 us (94%)
  local copies, waits for them, and re-layouts  2 us (4%)
  between operations  0.65 us (1%)
    pallas_call x1, Pallas kernels, body(): pl.pallas_call(functools.partial(kernel, sizes), out_shape=(jax.ShapeDtyp...  42 us
    unnamed x4, local copies, waits for them, and re-layouts  2 us

profile of v4, /device:TPU:0, one launch (start us, length us, event | category | flops | bytes accessed | tf_op | source)
XLA Modules:
  0.0 44.7 jit_solution(12318276194028973098)
XLA Ops:
  0.6 42.0 %shard_map.59 = (f32[2,4,8,128]{3,2,1,0:T(8,128)}, f32[2,4,8,128]{3,2,1,0:T(8,128)}) custom-call(f32[8,8,128]{2,1,0:T(8,128)} %bitcast.1, f32[3,4,8,128]{3,2,1,0:T(8,128)} %intra_hbm.1, f32[3,4,8,128]{3,2,1,0:T(8,128)} %extra_hbm.1, f32[4,8,128]{2,1,0:T(8,128)} %membrane_hbm.1), custom_call_target="tpu_custom_call" | custom-call | tf_op jit(solution)/shard_map/pallas_call | solution.py:490
  42.7 0.0 copy-start
  42.7 1.4 %copy.8 = f32[2,4,8,128]{3,2,1,0:T(8,128)} copy(f32[2,4,8,128]{3,2,1,0:T(8,128)} %get-tuple-element.4) | data formatting | bytes 65536
  44.1 0.0 copy-done
  44.1 0.6 %copy.9 = f32[2,4,8,128]{3,2,1,0:T(8,128)} copy(f32[2,4,8,128]{3,2,1,0:T(8,128)S(1)} %copy-done) | data formatting | bytes 65536
Async XLA Ops:
  42.7 1.4 %copy-start = (f32[2,4,8,128]{3,2,1,0:T(8,128)S(1)}, f32[2,4,8,128]{3,2,1,0:T(8,128)}, u32[]{:S(2)}) copy-start(f32[2,4,8,128]{3,2,1,0:T(8,128)} %get-tuple-element.5) | copy-start | bytes 98308
